TPU v7x, 32 devices: a whole 2x2x4 slice. The times are simulated.
32 devices in a mesh: expert: 4 (over x, core), shard: 8 (over z, y).
Axes of the slice: x: 2, y: 2, z: 4, core: 2. Of those that a mesh axis runs over, the one named last changes fastest.
Arguments:
- w_gate: float32 [64, 2048, 1408], P('expert', 'shard'), may hold values from -0.1875 to 0.1875
- w_up: float32 [64, 2048, 1408], P('expert', 'shard'), may hold values from -0.1875 to 0.1875
- router_weight: float32 [2048, 64], P('shard', 'expert'), may hold values from -0.125 to 0.125
- router_gain: float32 [2048], P('shard'), may hold values from 0.25 to 1.75
Outputs:
- serve_gate: bfloat16 [64, 2048, 1408], P('expert', None, 'shard')
- serve_up: bfloat16 [64, 2048, 1408], P('expert', None, 'shard')
- scale_gate: float32 [64, 1408], P('expert', 'shard')
- scale_up: float32 [64, 1408], P('expert', 'shard')
- serve_router: bfloat16 [2048, 64], replicated
All inputs are finite; a program needn't handle non-finite values. Where the computation divides by a largest or mean magnitude, that divisor is 1e-20 or more.
Results may differ from a plain program's by a relative error of at most 0.001.
Values may be sent and summed in bfloat16 or wider, within the bound.
A program may use at most 192 MiB of HBM per device.

v0:
```python
import functools

import jax
import jax.numpy as jnp
from jax import lax
from jax.experimental import pallas as pl
from jax.experimental.pallas import tpu as pltpu
from jax.sharding import PartitionSpec as P

LANES = 128
SLOTS = 2


def plain(w_gate, w_up, router_weight, router_gain):
    model = w_gate.shape[1] * lax.axis_size("shard")
    total_gate, total_up = lax.psum(
        (jnp.sum(jnp.abs(w_gate), axis=1), jnp.sum(jnp.abs(w_up), axis=1)), "shard"
    )
    served = []
    scales = []
    for w, total in ((w_gate, total_gate), (w_up, total_up)):
        scale = total / model
        narrow = (w / jnp.expand_dims(scale, 1)).astype(jnp.bfloat16)
        out = lax.all_to_all(narrow, "shard", split_axis=2, concat_axis=1, tiled=True)
        served.append(out)
        scales.append(
            lax.dynamic_slice_in_dim(
                scale, lax.axis_index("shard") * out.shape[2], out.shape[2], axis=1
            )
        )
    part_router = (router_weight * router_gain[:, None]).astype(jnp.bfloat16)
    row_router = lax.all_gather(part_router, "shard", axis=0, tiled=True)
    serve_router = lax.all_gather(row_router, "expert", axis=1, tiled=True)
    return (*served, *scales, serve_router)


def kernel(
    n, groups, model,
    part_ref, router_ref, gate_ref, up_ref,
    out_gate, out_up, scale_ref, out_router,
    stage, loaded, arrived, block,
    load_sem, own_sem, sum_send, sum_recv, mean_send, mean_recv,
    col_send, col_recv, row_send, row_recv, data_send, data_recv,
):
    me = lax.axis_index("shard")
    group = lax.axis_index("expert")
    tasks, tiles, _ = part_ref.shape
    experts, rows, width = gate_ref.shape
    columns = width // n
    share = tasks // n
    heads = router_ref.shape[0]

    def to(p):
        return lax.rem(me + p, n)

    def source(p):
        return lax.rem(me + n - p, n)

    def load(w_ref, e, slot):
        return pltpu.make_async_copy(w_ref.at[e], loaded.at[slot], load_sem.at[slot])

    load(gate_ref, 0, 0).start()

    barrier = pltpu.get_barrier_semaphore()
    for p in range(1, n):
        pl.semaphore_signal(barrier, inc=1, device_id={"shard": to(p)})
    for q in range(1, groups):
        pl.semaphore_signal(
            barrier, inc=1, device_id={"expert": lax.rem(group + q, groups)}
        )
    pl.semaphore_wait(barrier, n - 1 + groups - 1)

    sums = []
    for p in range(1, n):
        copy = pltpu.make_async_remote_copy(
            src_ref=part_ref.at[pl.ds(to(p) * share, share)],
            dst_ref=arrived.at[p],
            send_sem=sum_send.at[p],
            recv_sem=sum_recv.at[p],
            device_id={"shard": to(p)},
        )
        copy.start()
        sums.append(copy)

    mine = pl.ds(pl.multiple_of(group * heads, heads), heads)
    block[mine, :] = router_ref[...]
    cols = []
    for q in range(1, groups):
        copy = pltpu.make_async_remote_copy(
            src_ref=router_ref,
            dst_ref=block.at[mine],
            send_sem=col_send.at[q],
            recv_sem=col_recv.at[q],
            device_id={"expert": lax.rem(group + q, groups)},
        )
        copy.start()
        cols.append(copy)

    total = part_ref[pl.ds(me * share, share)]
    for p in range(1, n):
        sums[p - 1].wait_recv()
        total = total + arrived[p]
    own = pl.ds(me * share, share)
    scale_ref[own] = total / model
    means = []
    for p in range(1, n):
        copy = pltpu.make_async_remote_copy(
            src_ref=scale_ref.at[own],
            dst_ref=scale_ref.at[own],
            send_sem=mean_send.at[p],
            recv_sem=mean_recv.at[p],
            device_id={"shard": to(p)},
        )
        copy.start()
        means.append(copy)
    for copy in means:
        copy.wait_recv()

    my_rows = pl.ds(pl.multiple_of(me * rows, rows), rows)

    def piece(k):
        return pl.ds(pl.multiple_of(k * columns, 16), columns)

    order = list(range(1, n))
    for w, (w_ref, out) in enumerate(((gate_ref, out_gate), (up_ref, out_up))):

        def step(e, carry, w=w, w_ref=w_ref, out=out):
            slot = lax.rem(e, SLOTS)
            task = w * experts + e

            @pl.when(e + 1 < experts)
            def _():
                load(w_ref, e + 1, lax.rem(e + 1, SLOTS)).start()

            load(w_ref, e, slot).wait()
            for t in range(tiles):
                lanes = slice(t * LANES, (t + 1) * LANES)
                inverse = 1.0 / scale_ref[task, t : t + 1, :]
                scaled = loaded[slot, :, lanes] * inverse
                stage[task, lanes, :] = scaled.T.astype(jnp.bfloat16)
            for p in order:
                pltpu.make_async_remote_copy(
                    src_ref=stage.at[task, piece(to(p))],
                    dst_ref=out.at[e, :, my_rows],
                    send_sem=data_send.at[w, p],
                    recv_sem=data_recv.at[w, p],
                    device_id={"shard": to(p)},
                ).start()
            pltpu.make_async_copy(
                stage.at[task, piece(me)], out.at[e, :, my_rows], own_sem.at[w]
            ).start()
            return carry

        lax.fori_loop(0, experts, step, 0)
        if w == 0:
            load(up_ref, 0, 0).start()
            for copy in cols:
                copy.wait_recv()
            lines = []
            for p in range(1, n):
                copy = pltpu.make_async_remote_copy(
                    src_ref=block,
                    dst_ref=out_router.at[:, my_rows],
                    send_sem=row_send.at[p],
                    recv_sem=row_recv.at[p],
                    device_id={"shard": to(p)},
                )
                copy.start()
                lines.append(copy)
            out_router[:, my_rows] = block[...]

    for copy in sums + cols + means:
        copy.wait_send()
    for copy in lines:
        copy.wait()
    for w, out in enumerate((out_gate, out_up)):
        held = pl.ds(w * experts, experts)
        pltpu.make_async_copy(
            stage.at[held, piece(me)], out.at[:, :, my_rows], own_sem.at[w]
        ).wait()
        for p in range(1, n):
            from_p = pl.ds(pl.multiple_of(source(p) * rows, rows), rows)
            both = pltpu.make_async_remote_copy(
                src_ref=stage.at[held, piece(to(p))],
                dst_ref=out.at[:, :, from_p],
                send_sem=data_send.at[w, p],
                recv_sem=data_recv.at[w, p],
                device_id={"shard": to(p)},
            )
            both.wait_send()
            both.wait_recv()


def on_device(w_gate, w_up, router_weight, router_gain):
    n, groups = lax.axis_size("shard"), lax.axis_size("expert")
    experts, rows, width = w_gate.shape
    heads = router_weight.shape[1]
    tasks, columns, model = 2 * experts, width // n, rows * n
    if rows % LANES or width % LANES or columns % 16 or tasks % n or heads % 16:
        return plain(w_gate, w_up, router_weight, router_gain)
    tiles = width // LANES
    part = jnp.concatenate(
        [jnp.sum(jnp.abs(w_gate), axis=1), jnp.sum(jnp.abs(w_up), axis=1)]
    ).reshape(tasks, tiles, LANES)
    part_router = (router_weight * router_gain[:, None]).astype(jnp.bfloat16).T
    vmem = pl.BlockSpec(memory_space=pltpu.VMEM)
    hbm = pl.BlockSpec(memory_space=pl.ANY)
    dma = pltpu.SemaphoreType.DMA
    out_gate, out_up, scale, router = pl.pallas_call(
        functools.partial(kernel, n, groups, model),
        out_shape=(
            jax.ShapeDtypeStruct((experts, columns, model), jnp.bfloat16),
            jax.ShapeDtypeStruct((experts, columns, model), jnp.bfloat16),
            jax.ShapeDtypeStruct((tasks, tiles, LANES), jnp.float32),
            jax.ShapeDtypeStruct((heads * groups, model), jnp.bfloat16),
        ),
        in_specs=[vmem, vmem, hbm, hbm],
        out_specs=(hbm, hbm, vmem, vmem),
        scratch_shapes=[
            pltpu.VMEM((tasks, width, rows), jnp.bfloat16),
            pltpu.VMEM((SLOTS, rows, width), jnp.float32),
            pltpu.VMEM((n, tasks // n, tiles, LANES), jnp.float32),
            pltpu.VMEM((heads * groups, rows), jnp.bfloat16),
            dma((SLOTS,)),
            dma((2,)),
            dma((n,)), dma((n,)),
            dma((n,)), dma((n,)),
            dma((groups,)), dma((groups,)),
            dma((n,)), dma((n,)),
            dma((2, n)), dma((2, n)),
        ],
        compiler_params=pltpu.CompilerParams(
            collective_id=0, has_side_effects=True, vmem_limit_bytes=56 * 2**20
        ),
    )(part, part_router, w_gate, w_up)
    mine = lax.dynamic_slice_in_dim(
        scale.reshape(tasks, width), lax.axis_index("shard") * columns, columns, axis=1
    )
    return (
        out_gate.swapaxes(1, 2),
        out_up.swapaxes(1, 2),
        mine[:experts],
        mine[experts:],
        router.T,
    )


def solution(mesh):
    placed = (
        P("expert", "shard", None),
        P("expert", "shard", None),
        P("shard", "expert"),
        P("shard"),
    )
    return jax.shard_map(
        on_device,
        mesh=mesh,
        in_specs=placed,
        out_specs=(
            P("expert", None, "shard"),
            P("expert", None, "shard"),
            P("expert", "shard"),
            P("expert", "shard"),
            P(),
        ),
        check_vma=False,
    )
```

profile of v0, /device:TPU:0, one launch (start us, length us, event | category | flops | bytes accessed | tf_op | source)
XLA Modules:
  0.0 550.9 jit_solution(2449466871608512085)
XLA Ops:
  0.6 0.0 copy-start.1
  0.6 0.0 copy-start.2
  0.7 15.2 %abs_reduce_fusion = (f32[16,1408]{1,0:T(8,128)S(1)}, f32[16,1408]{1,0:T(8,128)S(1)}) fusion(f32[16,256,1408]{2,1,0:T(8,128)} %up_ref.1, f32[16,256,1408]{2,1,0:T(8,128)} %gate_ref.1), kind=kLoop, calls=%fused_computation | loop fusion | flops 23023616 | bytes 46317568 | tf_op jit(solution)/shard_map/reduce_sum | solution.py:203
  15.9 0.7 reshape.17.part_ref
  16.7 0.0 copy-done.1
  16.7 0.0 copy-done.2
  16.7 0.6 fusion.router_ref
  17.3 515.2 %shard_map.83 = (bf16[16,176,2048]{2,1,0:T(8,128)(2,1)}, bf16[16,176,2048]{2,1,0:T(8,128)(2,1)}, f32[32,11,128]{2,1,0:T(8,128)}, bf16[64,2048]{1,0:T(8,128)(2,1)}) custom-call(f32[32,11,128]{2,1,0:T(8,128)} %reshape.17.part_ref, bf16[16,256]{1,0:T(8,128)(2,1)} %fusion.router_ref, f32[16,256,1408]{2,1,0:T(8,128)} %gate_ref.1, f32[16,256,1408]{2,1,0:T(8,128)} %up_ref.1), custom_call_target="tpu_custom_call" | custom-call | tf_op jit(solution)/shard_map/pallas_call | solution.py:209
  532.5 0.0 slice-start
  532.5 1.2 copy.11
  533.7 0.7 fusion.1
  534.4 0.0 slice-start.1
  534.4 0.0 slice-start.2
  534.4 0.0 copy-start
  534.4 11.4 %copy.15 = bf16[16,2048,176]{1,2,0:T(8,128)(2,1)} copy(bf16[16,2048,176]{1,2,0:T(8,128)(2,1)} %bitcast.12) | data formatting | bytes 23068672
  545.8 0.0 slice-done
  545.8 0.0 slice-done.1
  545.8 0.0 slice-done.2
  545.8 4.4 copy.16
  550.2 0.0 copy-done
  550.2 0.7 copy.17
  (2 shorter events, 0.0 us)
Async XLA Ops:
  0.6 16.0 %copy-start.1 = (f32[256,16]{0,1:T(8,128)S(1)}, f32[256,16]{0,1:T(8,128)}, u32[]{:S(2)}) copy-start(f32[256,16]{0,1:T(8,128)} %param.6) | copy-start | bytes 49156
  0.6 16.0 %copy-start.2 = (f32[256]{0:T(256)S(1)}, f32[256]{0:T(256)}, u32[]{:S(2)}) copy-start(f32[256]{0:T(256)} %param.7) | copy-start | bytes 3076
  532.5 13.3 %slice-start = ((s8[11534336]{0:T(1024)(128)(4,1)}), s8[3145728]{0:T(1024)(128)(4,1)S(1)}, s32[]{:S(2)}) async-start(s8[11534336]{0:T(1024)(128)(4,1)} %bitcast.9), calls=%async_computation | async-start | bytes 6291456
  534.4 11.4 %slice-start.1 = ((s8[11534336]{0:T(1024)(128)(4,1)}), s8[4194304]{0:T(1024)(128)(4,1)S(1)}, s32[]{:S(2)}) async-start(s8[11534336]{0:T(1024)(128)(4,1)} %bitcast.9), calls=%async_computation.1 | async-start | bytes 8388608
  534.4 11.4 %slice-start.2 = ((s8[11534336]{0:T(1024)(128)(4,1)}), s8[4194304]{0:T(1024)(128)(4,1)S(1)}, s32[]{:S(2)}) async-start(s8[11534336]{0:T(1024)(128)(4,1)} %bitcast.9), calls=%async_computation.2 | async-start | bytes 8388608
  534.4 15.9 %copy-start = (bf16[64,2048]{1,0:T(8,128)(2,1)S(1)}, bf16[64,2048]{1,0:T(8,128)(2,1)}, u32[]{:S(2)}) copy-start(bf16[64,2048]{1,0:T(8,128)(2,1)} %get-tuple-element.12) | copy-start | bytes 786436
where the time goes:
time: 553 us; the launch traced here: 551 us
  Pallas kernels  515 us (93%)
  local copies, waits for them, and re-layouts  19.2 us (3%)
  other arithmetic  15.9 us (3%)
    pallas_call x1, Pallas kernels, on_device(): pl.pallas_call(functools.partial(kernel, n, groups, model), out_shape=(ja...  515 us
    unnamed x16, local copies, waits for them, and re-layouts  17.7 us
    reduce_sum x1, other arithmetic, on_device(): jnp.sum(jnp.abs(w_up), axis=1)  15.2 us

commit v1 on v0

v1 whole, which is shorter than its diff:
```python
import functools

import jax
import jax.numpy as jnp
from jax import lax
from jax.experimental import pallas as pl
from jax.experimental.pallas import tpu as pltpu
from jax.sharding import PartitionSpec as P

LANES = 128
SLOTS = 4
EARLY = 3
AHEAD = 12


def plain(w_gate, w_up, router_weight, router_gain):
    model = w_gate.shape[1] * lax.axis_size("shard")
    total_gate, total_up = lax.psum(
        (jnp.sum(jnp.abs(w_gate), axis=1), jnp.sum(jnp.abs(w_up), axis=1)), "shard"
    )
    served = []
    scales = []
    for w, total in ((w_gate, total_gate), (w_up, total_up)):
        scale = total / model
        narrow = (w / jnp.expand_dims(scale, 1)).astype(jnp.bfloat16)
        out = lax.all_to_all(narrow, "shard", split_axis=2, concat_axis=1, tiled=True)
        served.append(out)
        scales.append(
            lax.dynamic_slice_in_dim(
                scale, lax.axis_index("shard") * out.shape[2], out.shape[2], axis=1
            )
        )
    part_router = (router_weight * router_gain[:, None]).astype(jnp.bfloat16)
    row_router = lax.all_gather(part_router, "shard", axis=0, tiled=True)
    serve_router = lax.all_gather(row_router, "expert", axis=1, tiled=True)
    return (*served, *scales, serve_router)


def kernel(
    n, groups, model,
    weight_ref, gain_ref, gate_ref, up_ref,
    out_gate, out_up, scale_ref, out_router,
    stage, kept, loaded, part, quick, first, near_sum, far_sum, half_sum, raw, gains,
    load_sem, kept_sem, raw_sem, early_send, early_recv,
    near_send, near_recv, far_send, far_recv, mean_send, mean_recv,
    row_send, row_recv, col_send, col_recv, data_send, data_recv,
):
    me = lax.axis_index("shard")
    group = lax.axis_index("expert")
    experts, rows, width = gate_ref.shape
    tasks, tiles, _ = part.shape
    half = n // 2
    share = tasks // half
    columns = width // n
    heads = weight_ref.shape[0]
    later = tasks - EARLY
    side, spot = me // half, lax.rem(me, half)

    def sent_to(i):
        if i < half:
            return (1 - side) * half + lax.rem(spot + i, half)
        return side * half + lax.rem(spot + i - half + 1, half)

    def come_from(i):
        if i < half:
            return (1 - side) * half + lax.rem(spot + half - i, half)
        return side * half + lax.rem(spot + half - (i - half + 1), half)

    peers = range(n - 1)
    near = range(half, n - 1)

    def remote(src, dst, send, recv, shard=None, expert=None):
        return pltpu.make_async_remote_copy(
            src_ref=src, dst_ref=dst, send_sem=send, recv_sem=recv,
            device_id={"shard": shard} if expert is None else {"expert": expert},
        )

    def start_load(j):
        task, slot = EARLY + lax.rem(j, later), lax.rem(j, SLOTS)

        @pl.when((j < 2 * later) & (task < experts))
        def _():
            pltpu.make_async_copy(
                gate_ref.at[task], loaded.at[slot], load_sem.at[slot]
            ).start()

        @pl.when((j < 2 * later) & (task >= experts))
        def _():
            pltpu.make_async_copy(
                up_ref.at[task - experts], loaded.at[slot], load_sem.at[slot]
            ).start()

    def wait_load(slot):
        pltpu.make_async_copy(
            gate_ref.at[0], loaded.at[slot], load_sem.at[slot]
        ).wait()

    def keep(task):
        return pltpu.make_async_copy(
            gate_ref.at[task], kept.at[task], kept_sem.at[task]
        )

    def add_up(task, ref, slot):
        for t in range(tiles):
            lanes = slice(t * LANES, (t + 1) * LANES)
            part[task, t : t + 1, :] = jnp.sum(
                jnp.abs(ref[slot, :, lanes]), axis=0, keepdims=True
            )

    def add_later(j, carry):
        slot = lax.rem(j, SLOTS)
        wait_load(slot)
        add_up(EARLY + j, loaded, slot)
        start_load(j + SLOTS)
        return carry

    def shape_task(task, ref, slot, means, index):
        for t in range(tiles):
            lanes = slice(t * LANES, (t + 1) * LANES)
            inverse = 1.0 / means[index, t : t + 1, :]
            scaled = ref[slot, :, lanes] * inverse
            stage[task, lanes, :] = scaled.T.astype(jnp.bfloat16)

    my_rows = pl.ds(pl.multiple_of(me * rows, rows), rows)

    def piece(k):
        return pl.ds(pl.multiple_of(k * columns, 16), columns)

    def send_task(task, w, out, chosen):
        e = task - w * experts
        for i in chosen:
            remote(
                stage.at[task, piece(sent_to(i))],
                out.at[e, :, my_rows],
                data_send.at[w, i],
                data_recv.at[w, i],
                shard=sent_to(i),
            ).start()

    def keep_own(task, w, out):
        out[task - w * experts, :, my_rows] = stage[task, piece(me)]

    for task in range(EARLY):
        keep(task).start()
    fetch_weight = pltpu.make_async_copy(weight_ref, raw, raw_sem.at[0])
    fetch_gain = pltpu.make_async_copy(gain_ref, gains, raw_sem.at[1])
    fetch_weight.start()
    fetch_gain.start()
    for j in range(SLOTS):
        start_load(j)

    barrier = pltpu.get_barrier_semaphore()
    for i in peers:
        pl.semaphore_signal(barrier, inc=1, device_id={"shard": sent_to(i)})
    for q in range(1, groups):
        pl.semaphore_signal(
            barrier, inc=1, device_id={"expert": lax.rem(group + q, groups)}
        )

    started = []

    def begin(copy):
        copy.start()
        started.append(copy)
        return copy

    keep(0).wait()
    add_up(0, kept, 0)
    pl.semaphore_wait(barrier, n - 1 + groups - 1)

    early = []
    for i in peers:
        early.append(begin(remote(
            part.at[pl.ds(0, 1)], first.at[me, pl.ds(0, 1)],
            early_send.at[0, i], early_recv.at[0, i], shard=sent_to(i),
        )))
    first[me, 0:1] = part[0:1]
    for task in range(1, EARLY):
        keep(task).wait()
        add_up(task, kept, task)
    rest = []
    for i in peers:
        rest.append(begin(remote(
            part.at[pl.ds(1, EARLY - 1)], first.at[me, pl.ds(1, EARLY - 1)],
            early_send.at[1, i], early_recv.at[1, i], shard=sent_to(i),
        )))
    first[me, 1:EARLY] = part[1:EARLY]

    fetch_weight.wait()
    fetch_gain.wait()
    mine = pl.ds(pl.multiple_of(group * heads, heads), heads)
    out_router[mine, my_rows] = (raw[...] * gains[...]).astype(jnp.bfloat16)
    lines = []
    for i in peers:
        lines.append(begin(remote(
            out_router.at[mine, my_rows], out_router.at[mine, my_rows],
            row_send.at[i], row_recv.at[i], shard=sent_to(i),
        )))

    lax.fori_loop(0, AHEAD, add_later, 0)

    def early_mean(lo, hi):
        total = first[0, lo:hi]
        for s in range(1, n):
            total = total + first[s, lo:hi]
        quick[lo:hi] = total / model

    for copy in early:
        copy.wait_recv()
    early_mean(0, 1)
    shape_task(0, kept, 0, quick, 0)
    send_task(0, 0, out_gate, peers)

    lax.fori_loop(AHEAD, later, add_later, 0)

    sums = []
    for i in near:
        sums.append(begin(remote(
            part.at[pl.ds(sent_to(i) % half * share, share)],
            near_sum.at[i - half],
            near_send.at[i - half], near_recv.at[i - half], shard=sent_to(i),
        )))
    keep_own(0, 0, out_gate)
    for copy in rest:
        copy.wait_recv()
    early_mean(1, EARLY)
    shape_task(1, kept, 1, quick, 1)
    send_task(1, 0, out_gate, range(half // 2))

    own = pl.ds(spot * share, share)
    total = part[own]
    for i, copy in zip(near, sums):
        copy.wait_recv()
        total = total + near_sum[i - half]
    half_sum[...] = total
    across = begin(remote(
        half_sum, far_sum, far_send, far_recv, shard=sent_to(0)
    ))
    send_task(1, 0, out_gate, range(half // 2, n - 1))
    keep_own(1, 0, out_gate)

    for task in range(2, EARLY):
        shape_task(task, kept, task, quick, task)
    across.wait_recv()
    scale_ref[own] = (half_sum[...] + far_sum[...]) / model
    means = []
    for i in near:
        means.append(begin(remote(
            scale_ref.at[own], scale_ref.at[own],
            mean_send.at[i - half], mean_recv.at[i - half], shard=sent_to(i),
        )))
    for task in range(2, EARLY):
        send_task(task, 0, out_gate, peers)
        keep_own(task, 0, out_gate)

    for copy in lines:
        copy.wait_recv()
    cols = []
    for q in range(1, groups):
        cols.append(begin(remote(
            out_router.at[mine], out_router.at[mine],
            col_send.at[q], col_recv.at[q], expert=lax.rem(group + q, groups),
        )))
    for copy in means:
        copy.wait_recv()

    for w, out in enumerate((out_gate, out_up)):

        def step(task, carry, w=w, out=out):
            j = later + task - EARLY
            slot = lax.rem(j, SLOTS)
            wait_load(slot)
            shape_task(task, loaded, slot, scale_ref, task)
            send_task(task, w, out, peers)
            keep_own(task, w, out)
            start_load(j + SLOTS)
            return carry

        lax.fori_loop(max(EARLY, w * experts), (w + 1) * experts, step, 0)

    for copy in cols:
        copy.wait_recv()
    for copy in started:
        copy.wait_send()
    for w, out in enumerate((out_gate, out_up)):
        held = pl.ds(w * experts, experts)
        for i in peers:
            from_i = pl.ds(pl.multiple_of(come_from(i) * rows, rows), rows)
            both = remote(
                stage.at[held, piece(sent_to(i))], out.at[:, :, from_i],
                data_send.at[w, i], data_recv.at[w, i], shard=sent_to(i),
            )
            both.wait_send()
            both.wait_recv()


def settle(count, *refs):
    sources, outs, sem = refs[:count], refs[count : 2 * count], refs[-1]
    copies = [
        pltpu.make_async_copy(src, dst, sem.at[i])
        for i, (src, dst) in enumerate(zip(sources, outs))
    ]
    for copy in copies:
        copy.start()
    for copy in copies:
        copy.wait()


def on_device(w_gate, w_up, router_weight, router_gain):
    n, groups = lax.axis_size("shard"), lax.axis_size("expert")
    experts, rows, width = w_gate.shape
    heads = router_weight.shape[1]
    tasks, columns, model = 2 * experts, width // n, rows * n
    if (
        n % 2
        or n < 4
        or rows % LANES
        or width % LANES
        or columns % 16
        or heads % 16
        or tasks % (n // 2)
        or experts < EARLY + AHEAD
    ):
        return plain(w_gate, w_up, router_weight, router_gain)
    tiles, half = width // LANES, n // 2
    share = tasks // half
    hbm = pl.BlockSpec(memory_space=pl.ANY)
    vmem = pl.BlockSpec(memory_space=pltpu.VMEM)
    dma = pltpu.SemaphoreType.DMA
    held = (
        ((experts, columns, model), jnp.bfloat16),
        ((experts, columns, model), jnp.bfloat16),
        ((tasks, tiles, LANES), jnp.float32),
        ((heads * groups, model), jnp.bfloat16),
    )
    block = (share, tiles, LANES)
    arrived = pl.pallas_call(
        functools.partial(kernel, n, groups, model),
        out_shape=tuple(pltpu.VMEM(*a) for a in held),
        in_specs=[hbm] * 4,
        out_specs=(vmem,) * 4,
        scratch_shapes=[
            pltpu.VMEM((tasks, width, rows), jnp.bfloat16),
            pltpu.VMEM((EARLY, rows, width), jnp.float32),
            pltpu.VMEM((SLOTS, rows, width), jnp.float32),
            pltpu.VMEM((tasks, tiles, LANES), jnp.float32),
            pltpu.VMEM((EARLY, tiles, LANES), jnp.float32),
            pltpu.VMEM((n, EARLY, tiles, LANES), jnp.float32),
            pltpu.VMEM((half - 1, *block), jnp.float32),
            pltpu.VMEM(block, jnp.float32),
            pltpu.VMEM(block, jnp.float32),
            pltpu.VMEM((heads, rows), jnp.float32),
            pltpu.VMEM((1, rows), jnp.float32),
            dma((SLOTS,)), dma((EARLY,)), dma((2,)),
            dma((2, n - 1)), dma((2, n - 1)),
            dma((half - 1,)), dma((half - 1,)),
            dma, dma,
            dma((half - 1,)), dma((half - 1,)),
            dma((n - 1,)), dma((n - 1,)),
            dma((groups,)), dma((groups,)),
            dma((2, n - 1)), dma((2, n - 1)),
        ],
        compiler_params=pltpu.CompilerParams(
            collective_id=0, has_side_effects=True, vmem_limit_bytes=38 * 2**20
        ),
    )(router_weight.T, router_gain[None, :], w_gate, w_up)
    out_gate, out_up, scale, router = pl.pallas_call(
        functools.partial(settle, len(held)),
        out_shape=tuple(jax.ShapeDtypeStruct(*a) for a in held),
        in_specs=[vmem] * len(held),
        out_specs=(hbm,) * len(held),
        scratch_shapes=[dma((len(held),))],
        compiler_params=pltpu.CompilerParams(vmem_limit_bytes=2**20),
    )(*arrived)
    mine = lax.dynamic_slice_in_dim(
        scale.reshape(tasks, width), lax.axis_index("shard") * columns, columns, axis=1
    )
    return (
        out_gate.swapaxes(1, 2),
        out_up.swapaxes(1, 2),
        mine[:experts],
        mine[experts:],
        router.T,
    )


def solution(mesh):
    placed = (
        P("expert", "shard", None),
        P("expert", "shard", None),
        P("shard", "expert"),
        P("shard"),
    )
    return jax.shard_map(
        on_device,
        mesh=mesh,
        in_specs=placed,
        out_specs=(
            P("expert", None, "shard"),
            P("expert", None, "shard"),
            P("expert", "shard"),
            P("expert", "shard"),
            P(),
        ),
        check_vma=False,
    )
```

time: 553 us -> 522 us (0.944)
  local copies, waits for them, and re-layouts: 19.2 us -> 0.76 us
  other arithmetic: 15.9 us -> 0 us
  Pallas kernels: 515 us -> 521 us
    unnamed x16 -> x1, local copies, waits for them, and re-layouts: 17.7 us -> 0.06 us
    reduce_sum x1 -> x0, other arithmetic: 15.2 us -> none  [on_device(): jnp.sum(jnp.abs(w_up), axis=1)]
    pallas_call x1 -> x2, Pallas kernels: 515 us -> 521 us  [the longest x1 513 us: on_device(): pl.pallas_call(functools.partial(kernel, n, groups, model), out_shape=tup...]
where the time goes in v1:
time: 522 us
  Pallas kernels  521 us (100%)
    pallas_call x1, Pallas kernels, on_device(): pl.pallas_call(functools.partial(kernel, n, groups, model), out_shape=tup...  513 us

profile of v1, /device:TPU:0, one launch (start us, length us, event | category | flops | bytes accessed | tf_op | source)
XLA Modules:
  0.0 522.2 jit_solution(6674062235150531399)
XLA Ops:
  0.6 512.6 %shard_map.83 = (bf16[16,176,2048]{2,1,0:T(8,128)(2,1)S(1)}, bf16[16,176,2048]{2,1,0:T(8,128)(2,1)S(1)}, f32[32,11,128]{2,1,0:T(8,128)S(1)}, bf16[64,2048]{1,0:T(8,128)(2,1)S(1)}) custom-call(f32[16,256]{1,0:T(8,128)} %bitcast.11, f32[1,256]{1,0:T(1,128)} %bitcast.12, f32[16,256,1408]{2,1,0:T(8,128)} %gate_ref.1, f32[16,256,1408]{2,1,0:T(8,128)} %up_ref.1), custom_call_target="tpu_custom_call" | custom-call | tf_op jit(solution)/shard_map/pallas_call | solution.py:337
  513.2 8.3 %shard_map.84 = (bf16[16,176,2048]{2,1,0:T(8,128)(2,1)}, bf16[16,176,2048]{2,1,0:T(8,128)(2,1)}, f32[32,11,128]{2,1,0:T(8,128)S(1)}, bf16[64,2048]{1,0:T(8,128)(2,1)}) custom-call(bf16[16,176,2048]{2,1,0:T(8,128)(2,1)S(1)} %get-tuple-element.13.refs_0_, bf16[16,176,2048]{2,1,0:T(8,128)(2,1)S(1)} %get-tuple-element.14.refs_1_, ...), custom_call_target="tpu_custom_call" | custom-call | tf_op jit(solution)/shard_map/pallas_call | solution.py:367
  521.5 0.1 copy.11
  521.5 0.7 fusion

commit v2 on v1

--- a/solution.py
+++ b/solution.py
@@ -10,7 +10,9 @@
 LANES = 128
 SLOTS = 4
 EARLY = 3
-AHEAD = 12
+AHEAD = 2
+PARTS = 8
+LEAD = 3
 
 
 def plain(w_gate, w_up, router_weight, router_gain):
@@ -39,8 +41,8 @@
 def kernel(
     n, groups, model,
     weight_ref, gain_ref, gate_ref, up_ref,
-    out_gate, out_up, scale_ref, out_router,
-    stage, kept, loaded, part, quick, first, near_sum, far_sum, half_sum, raw, gains,
+    out_gate, out_up, gate_scale, up_scale, out_router,
+    scale_ref, stage, kept, loaded, part, quick, first, near_sum, far_sum, half_sum, raw, gains,
     load_sem, kept_sem, raw_sem, early_send, early_recv,
     near_send, near_recv, far_send, far_recv, mean_send, mean_recv,
     row_send, row_recv, col_send, col_recv, data_send, data_recv,
@@ -56,18 +58,19 @@
     later = tasks - EARLY
     side, spot = me // half, lax.rem(me, half)
 
+    peers = range(n - 1)
+    near = range(half - 1)
+
     def sent_to(i):
-        if i < half:
-            return (1 - side) * half + lax.rem(spot + i, half)
-        return side * half + lax.rem(spot + i - half + 1, half)
+        return lax.rem(me + i + 1, n)
 
     def come_from(i):
-        if i < half:
-            return (1 - side) * half + lax.rem(spot + half - i, half)
-        return side * half + lax.rem(spot + half - (i - half + 1), half)
-
-    peers = range(n - 1)
-    near = range(half, n - 1)
+        return lax.rem(me + n - i - 1, n)
+
+    def beside(i):
+        return side * half + lax.rem(spot + i + 1, half)
+
+    across = lax.rem(me + half, n)
 
     def remote(src, dst, send, recv, shard=None, expert=None):
         return pltpu.make_async_remote_copy(
@@ -216,38 +219,35 @@
     sums = []
     for i in near:
         sums.append(begin(remote(
-            part.at[pl.ds(sent_to(i) % half * share, share)],
-            near_sum.at[i - half],
-            near_send.at[i - half], near_recv.at[i - half], shard=sent_to(i),
+            part.at[pl.ds(lax.rem(beside(i), half) * share, share)],
+            near_sum.at[i], near_send.at[i], near_recv.at[i], shard=beside(i),
         )))
     keep_own(0, 0, out_gate)
     for copy in rest:
         copy.wait_recv()
     early_mean(1, EARLY)
     shape_task(1, kept, 1, quick, 1)
-    send_task(1, 0, out_gate, range(half // 2))
+    send_task(1, 0, out_gate, range(LEAD))
 
     own = pl.ds(spot * share, share)
     total = part[own]
     for i, copy in zip(near, sums):
         copy.wait_recv()
-        total = total + near_sum[i - half]
+        total = total + near_sum[i]
     half_sum[...] = total
-    across = begin(remote(
-        half_sum, far_sum, far_send, far_recv, shard=sent_to(0)
-    ))
-    send_task(1, 0, out_gate, range(half // 2, n - 1))
+    crossing = begin(remote(half_sum, far_sum, far_send, far_recv, shard=across))
+    send_task(1, 0, out_gate, range(LEAD, n - 1))
     keep_own(1, 0, out_gate)
 
     for task in range(2, EARLY):
         shape_task(task, kept, task, quick, task)
-    across.wait_recv()
+    crossing.wait_recv()
     scale_ref[own] = (half_sum[...] + far_sum[...]) / model
     means = []
     for i in near:
         means.append(begin(remote(
             scale_ref.at[own], scale_ref.at[own],
-            mean_send.at[i - half], mean_recv.at[i - half], shard=sent_to(i),
+            mean_send.at[i], mean_recv.at[i], shard=beside(i),
         )))
     for task in range(2, EARLY):
         send_task(task, 0, out_gate, peers)
@@ -263,6 +263,18 @@
         )))
     for copy in means:
         copy.wait_recv()
+
+    for k in range(n):
+
+        @pl.when(me == k)
+        def _(k=k):
+            lo = k * columns
+            for t in range(lo // LANES, (lo + columns - 1) // LANES + 1):
+                left = max(lo, t * LANES)
+                right = min(lo + columns, (t + 1) * LANES)
+                seen = scale_ref[:, t, left - t * LANES : right - t * LANES]
+                gate_scale[:, left - lo : right - lo] = seen[:experts]
+                up_scale[:, left - lo : right - lo] = seen[experts:]
 
     for w, out in enumerate((out_gate, out_up)):
 
@@ -296,10 +308,15 @@
 
 def settle(count, *refs):
     sources, outs, sem = refs[:count], refs[count : 2 * count], refs[-1]
-    copies = [
-        pltpu.make_async_copy(src, dst, sem.at[i])
-        for i, (src, dst) in enumerate(zip(sources, outs))
-    ]
+    copies = []
+    for i, (src, dst) in enumerate(zip(sources, outs)):
+        parts = PARTS if src.ndim == 3 and src.shape[0] % PARTS == 0 else 1
+        step = src.shape[0] // parts
+        for k in range(parts):
+            rows = pl.ds(k * step, step)
+            copies.append(
+                pltpu.make_async_copy(src.at[rows], dst.at[rows], sem.at[i, k])
+            )
     for copy in copies:
         copy.start()
     for copy in copies:
@@ -330,7 +347,8 @@
     held = (
         ((experts, columns, model), jnp.bfloat16),
         ((experts, columns, model), jnp.bfloat16),
-        ((tasks, tiles, LANES), jnp.float32),
+        ((experts, columns), jnp.float32),
+        ((experts, columns), jnp.float32),
         ((heads * groups, model), jnp.bfloat16),
     )
     block = (share, tiles, LANES)
@@ -338,8 +356,9 @@
         functools.partial(kernel, n, groups, model),
         out_shape=tuple(pltpu.VMEM(*a) for a in held),
         in_specs=[hbm] * 4,
-        out_specs=(vmem,) * 4,
+        out_specs=(vmem,) * len(held),
         scratch_shapes=[
+            pltpu.VMEM((tasks, tiles, LANES), jnp.float32),
             pltpu.VMEM((tasks, width, rows), jnp.bfloat16),
             pltpu.VMEM((EARLY, rows, width), jnp.float32),
             pltpu.VMEM((SLOTS, rows, width), jnp.float32),
@@ -364,22 +383,19 @@
             collective_id=0, has_side_effects=True, vmem_limit_bytes=38 * 2**20
         ),
     )(router_weight.T, router_gain[None, :], w_gate, w_up)
-    out_gate, out_up, scale, router = pl.pallas_call(
+    out_gate, out_up, gate_scale, up_scale, router = pl.pallas_call(
         functools.partial(settle, len(held)),
         out_shape=tuple(jax.ShapeDtypeStruct(*a) for a in held),
         in_specs=[vmem] * len(held),
         out_specs=(hbm,) * len(held),
-        scratch_shapes=[dma((len(held),))],
+        scratch_shapes=[dma((len(held), PARTS))],
         compiler_params=pltpu.CompilerParams(vmem_limit_bytes=2**20),
     )(*arrived)
-    mine = lax.dynamic_slice_in_dim(
-        scale.reshape(tasks, width), lax.axis_index("shard") * columns, columns, axis=1
-    )
     return (
         out_gate.swapaxes(1, 2),
         out_up.swapaxes(1, 2),
-        mine[:experts],
-        mine[experts:],
+        gate_scale,
+        up_scale,
         router.T,
     )
 

time: 522 us -> 516 us (0.989)
  Pallas kernels: 521 us -> 513 us
    pallas_call x1, Pallas kernels: 513 us -> 505 us  [on_device(): pl.pallas_call(functools.partial(kernel, n, groups, model), out_shape=tup...]
where the time goes in v2:
time: 516 us; the launch traced here: 514 us
  Pallas kernels  513 us (99%)
    pallas_call x1, Pallas kernels, on_device(): pl.pallas_call(functools.partial(kernel, n, groups, model), out_shape=tup...  505 us

profile of v2, /device:TPU:0, one launch (start us, length us, event | category | flops | bytes accessed | tf_op | source)
XLA Modules:
  0.0 513.8 jit_solution(9865124927945813599)
XLA Ops:
  0.6 505.1 %shard_map.83 = (bf16[16,176,2048]{2,1,0:T(8,128)(2,1)S(1)}, bf16[16,176,2048]{2,1,0:T(8,128)(2,1)S(1)}, f32[16,176]{1,0:T(8,128)S(1)}, f32[16,176]{1,0:T(8,128)S(1)}, bf16[64,2048]{1,0:T(8,128)(2,1)S(1)}) custom-call(f32[16,256]{1,0:T(8,128)} %bitcast.5, f32[1,256]{1,0:T(1,128)} %bitcast.6, f32[16,256,1408]{2,1,0:T(8,128)} %gate_ref.1, f32[16,256,1408]{2,1,0:T(8,128)} %up_ref.1), custom_call_target="tpu_custom_call" | custom-call | tf_op jit(solution)/shard_map/pallas_call | solution.py:355
  505.7 8.1 %shard_map.84 = (bf16[16,176,2048]{2,1,0:T(8,128)(2,1)}, bf16[16,176,2048]{2,1,0:T(8,128)(2,1)}, f32[16,176]{1,0:T(8,128)}, f32[16,176]{1,0:T(8,128)}, bf16[64,2048]{1,0:T(8,128)(2,1)}) custom-call(bf16[16,176,2048]{2,1,0:T(8,128)(2,1)S(1)} %get-tuple-element.15.refs_0_, bf16[16,176,2048]{2,1,0:T(8,128)(2,1)S(1)} %get-tuple-element.16.refs_1_, ...), custom_call_target="tpu_custom_call" | custom-call | tf_op jit(solution)/shard_map/pallas_call | solution.py:386

commit v3 on v2

--- a/solution.py
+++ b/solution.py
@@ -13,6 +13,7 @@
 AHEAD = 2
 PARTS = 8
 LEAD = 3
+HELD = 3
 
 
 def plain(w_gate, w_up, router_weight, router_gain):
@@ -41,11 +42,11 @@
 def kernel(
     n, groups, model,
     weight_ref, gain_ref, gate_ref, up_ref,
-    out_gate, out_up, gate_scale, up_scale, out_router,
+    out_gate, out_up, gate_scale, up_scale, out_router, out_held,
     scale_ref, stage, kept, loaded, part, quick, first, near_sum, far_sum, half_sum, raw, gains,
     load_sem, kept_sem, raw_sem, early_send, early_recv,
     near_send, near_recv, far_send, far_recv, mean_send, mean_recv,
-    row_send, row_recv, col_send, col_recv, data_send, data_recv,
+    row_send, row_recv, col_send, col_recv, data_send, data_recv, held_sem,
 ):
     me = lax.axis_index("shard")
     group = lax.axis_index("expert")
@@ -278,32 +279,55 @@
 
     for w, out in enumerate((out_gate, out_up)):
 
-        def step(task, carry, w=w, out=out):
+        def step(task, carry, w=w, out=out, chosen=peers):
             j = later + task - EARLY
             slot = lax.rem(j, SLOTS)
             wait_load(slot)
             shape_task(task, loaded, slot, scale_ref, task)
-            send_task(task, w, out, peers)
+            send_task(task, w, out, chosen)
             keep_own(task, w, out)
             start_load(j + SLOTS)
             return carry
 
-        lax.fori_loop(max(EARLY, w * experts), (w + 1) * experts, step, 0)
+        stop = (w + 1) * experts - (HELD if w else 0)
+        lax.fori_loop(max(EARLY, w * experts), stop, step, 0)
+
+    fewer = functools.partial(step, chosen=[i for i in peers if i != half - 1])
+    lax.fori_loop(tasks - HELD, tasks, fewer, 0)
+    holding = pltpu.make_async_copy(
+        stage.at[pl.ds(tasks - HELD, HELD), piece(across)], out_held, held_sem
+    )
+    holding.start()
 
     for copy in cols:
         copy.wait_recv()
     for copy in started:
         copy.wait_send()
     for w, out in enumerate((out_gate, out_up)):
-        held = pl.ds(w * experts, experts)
         for i in peers:
+            count = experts - (HELD if w and i == half - 1 else 0)
+            held = pl.ds(w * experts, count)
             from_i = pl.ds(pl.multiple_of(come_from(i) * rows, rows), rows)
             both = remote(
-                stage.at[held, piece(sent_to(i))], out.at[:, :, from_i],
+                stage.at[held, piece(sent_to(i))], out.at[pl.ds(0, count), :, from_i],
                 data_send.at[w, i], data_recv.at[w, i], shard=sent_to(i),
             )
             both.wait_send()
             both.wait_recv()
+    holding.wait()
+
+
+def place(count, n, up_ref, got_ref, out_ref, sem):
+    me = lax.axis_index("shard")
+    experts, _, model = up_ref.shape
+    rows = model // n
+    across = lax.rem(me + n // 2, n)
+    there = pl.ds(pl.multiple_of(across * rows, rows), rows)
+    copy = pltpu.make_async_copy(
+        got_ref, out_ref.at[pl.ds(experts - count, count), :, there], sem
+    )
+    copy.start()
+    copy.wait()
 
 
 def settle(count, *refs):
@@ -352,11 +376,14 @@
         ((heads * groups, model), jnp.bfloat16),
     )
     block = (share, tiles, LANES)
-    arrived = pl.pallas_call(
+    *arrived, kept_back = pl.pallas_call(
         functools.partial(kernel, n, groups, model),
-        out_shape=tuple(pltpu.VMEM(*a) for a in held),
+        out_shape=(
+            *(pltpu.VMEM(*a) for a in held),
+            jax.ShapeDtypeStruct((HELD, columns, rows), jnp.bfloat16),
+        ),
         in_specs=[hbm] * 4,
-        out_specs=(vmem,) * len(held),
+        out_specs=(vmem,) * len(held) + (hbm,),
         scratch_shapes=[
             pltpu.VMEM((tasks, tiles, LANES), jnp.float32),
             pltpu.VMEM((tasks, width, rows), jnp.bfloat16),
@@ -377,20 +404,35 @@
             dma((half - 1,)), dma((half - 1,)),
             dma((n - 1,)), dma((n - 1,)),
             dma((groups,)), dma((groups,)),
-            dma((2, n - 1)), dma((2, n - 1)),
+            dma((2, n - 1)), dma((2, n - 1)), dma,
         ],
         compiler_params=pltpu.CompilerParams(
             collective_id=0, has_side_effects=True, vmem_limit_bytes=38 * 2**20
         ),
     )(router_weight.T, router_gain[None, :], w_gate, w_up)
+    swapped = lax.ppermute(
+        kept_back, "shard", [(s, (s + half) % n) for s in range(n)]
+    )
     out_gate, out_up, gate_scale, up_scale, router = pl.pallas_call(
         functools.partial(settle, len(held)),
         out_shape=tuple(jax.ShapeDtypeStruct(*a) for a in held),
         in_specs=[vmem] * len(held),
         out_specs=(hbm,) * len(held),
         scratch_shapes=[dma((len(held), PARTS))],
+        cost_estimate=pl.CostEstimate(
+            flops=4 * 10**8, bytes_accessed=8 * w_gate.size, transcendentals=0
+        ),
         compiler_params=pltpu.CompilerParams(vmem_limit_bytes=2**20),
     )(*arrived)
+    out_up = pl.pallas_call(
+        functools.partial(place, HELD, n),
+        out_shape=jax.ShapeDtypeStruct(out_up.shape, out_up.dtype),
+        in_specs=[hbm, hbm],
+        out_specs=hbm,
+        scratch_shapes=[dma],
+        input_output_aliases={0: 0},
+        compiler_params=pltpu.CompilerParams(vmem_limit_bytes=2**20),
+    )(out_up, swapped)
     return (
         out_gate.swapaxes(1, 2),
         out_up.swapaxes(1, 2),

time: 516 us -> 511 us (level)
  Pallas kernels: 513 us -> 504 us
    pallas_call x1 -> x2, Pallas kernels: 505 us -> 496 us  [the longest x1 495 us: on_device(): pl.pallas_call(functools.partial(kernel, n, groups, model), out_shape=(*(...]
  transfers between devices with their start and end apart: 0 -> 1, of which waited for: 0 -> 1; matrix products, arithmetic and copies ran while one was open for 0% -> 0% of each run, Pallas kernels for 0% -> 2%
where the time goes in v3:
time: 511 us
  Pallas kernels  504 us (99%)
    pallas_call x1, Pallas kernels, on_device(): pl.pallas_call(functools.partial(kernel, n, groups, model), out_shape=(*(...  495 us
  transfers between devices with their start and end apart: 1, of which 1 were waited for; matrix products, arithmetic and copies ran while one was open for 0% of the time, Pallas kernels for 2%

profile of v3, /device:TPU:0, one launch (start us, length us, event | category | flops | bytes accessed | tf_op | source)
XLA Modules:
  0.0 511.0 jit_solution(6669275225861528992)
XLA Ops:
  0.6 495.4 %shard_map.83 = (bf16[16,176,2048]{2,1,0:T(8,128)(2,1)S(1)}, bf16[16,176,2048]{2,1,0:T(8,128)(2,1)S(1)}, f32[16,176]{1,0:T(8,128)S(1)}, f32[16,176]{1,0:T(8,128)...) custom-call(f32[16,256]{1,0:T(8,128)} %bitcast.6, f32[1,256]{1,0:T(1,128)} %bitcast.7, ...), custom_call_target="tpu_custom_call" | custom-call | tf_op jit(solution)/shard_map/pallas_call | solution.py:379
  496.1 1.9 collective-permute-start
  498.0 8.1 %shard_map.84 = (bf16[16,176,2048]{2,1,0:T(8,128)(2,1)}, bf16[16,176,2048]{2,1,0:T(8,128)(2,1)}, f32[16,176]{1,0:T(8,128)}, f32[16,176]{1,0:T(8,128)}, bf16[64,2048]{1,0:T(8,128)(2,1)}) custom-call(bf16[16,176,2048]{2,1,0:T(8,128)(2,1)S(1)} %get-tuple-element.16.refs_0_, bf16[16,176,2048]{2,1,0:T(8,128)(2,1)S(1)} %get-tuple-element.17.refs_1_, ...), custom_call_target="tpu_custom_call" | custom-call | flops 400000000 | bytes 46137344 | tf_op jit(solution)/shard_map/pallas_call | solution.py:416
  506.1 4.2 collective-permute-done.got_ref
  510.3 0.7 shard_map.85
Async XLA Ops:
  496.1 14.2 %collective-permute-start = (bf16[3,176,256]{2,1,0:T(8,128)(2,1)}, bf16[3,176,256]{2,1,0:T(8,128)(2,1)S(1)}, u32[]{:S(2)}, u32[]{:S(2)}) collective-permute-start(bf16[3,176,256]{2,1,0:T(8,128)(2,1)} %get-tuple-element.23), channel_id=1, source_target_pairs={{0,4},{1,5},{2,6},{3,7},{4,0},{5,1},{6,2},{7,3},{8,12},{9,13},{10,... | collective-permute-start | bytes 811016 | tf_op jit(solution)/shard_map/ppermute | solution.py:413

commit v4 on v3

--- a/solution.py
+++ b/solution.py
@@ -10,7 +10,7 @@
 LANES = 128
 SLOTS = 4
 EARLY = 3
-AHEAD = 2
+AHEAD = 3
 PARTS = 8
 LEAD = 3
 HELD = 3
@@ -46,7 +46,7 @@
     scale_ref, stage, kept, loaded, part, quick, first, near_sum, far_sum, half_sum, raw, gains,
     load_sem, kept_sem, raw_sem, early_send, early_recv,
     near_send, near_recv, far_send, far_recv, mean_send, mean_recv,
-    row_send, row_recv, col_send, col_recv, data_send, data_recv, held_sem,
+    row_send, row_recv, col_send, col_recv, data_send, data_recv,
 ):
     me = lax.axis_index("shard")
     group = lax.axis_index("expert")
@@ -144,14 +144,9 @@
     def keep_own(task, w, out):
         out[task - w * experts, :, my_rows] = stage[task, piece(me)]
 
-    for task in range(EARLY):
-        keep(task).start()
+    keep(0).start()
     fetch_weight = pltpu.make_async_copy(weight_ref, raw, raw_sem.at[0])
     fetch_gain = pltpu.make_async_copy(gain_ref, gains, raw_sem.at[1])
-    fetch_weight.start()
-    fetch_gain.start()
-    for j in range(SLOTS):
-        start_load(j)
 
     barrier = pltpu.get_barrier_semaphore()
     for i in peers:
@@ -169,6 +164,12 @@
         return copy
 
     keep(0).wait()
+    for task in range(1, EARLY):
+        keep(task).start()
+    fetch_weight.start()
+    fetch_gain.start()
+    for j in range(SLOTS):
+        start_load(j)
     add_up(0, kept, 0)
     pl.semaphore_wait(barrier, n - 1 + groups - 1)
 
@@ -294,10 +295,7 @@
 
     fewer = functools.partial(step, chosen=[i for i in peers if i != half - 1])
     lax.fori_loop(tasks - HELD, tasks, fewer, 0)
-    holding = pltpu.make_async_copy(
-        stage.at[pl.ds(tasks - HELD, HELD), piece(across)], out_held, held_sem
-    )
-    holding.start()
+    out_held[...] = stage[pl.ds(tasks - HELD, HELD), piece(across)]
 
     for copy in cols:
         copy.wait_recv()
@@ -314,7 +312,6 @@
             )
             both.wait_send()
             both.wait_recv()
-    holding.wait()
 
 
 def place(count, n, up_ref, got_ref, out_ref, sem):
@@ -380,10 +377,10 @@
         functools.partial(kernel, n, groups, model),
         out_shape=(
             *(pltpu.VMEM(*a) for a in held),
-            jax.ShapeDtypeStruct((HELD, columns, rows), jnp.bfloat16),
+            pltpu.VMEM((HELD, columns, rows), jnp.bfloat16),
         ),
         in_specs=[hbm] * 4,
-        out_specs=(vmem,) * len(held) + (hbm,),
+        out_specs=(vmem,) * (len(held) + 1),
         scratch_shapes=[
             pltpu.VMEM((tasks, tiles, LANES), jnp.float32),
             pltpu.VMEM((tasks, width, rows), jnp.bfloat16),
@@ -404,7 +401,7 @@
             dma((half - 1,)), dma((half - 1,)),
             dma((n - 1,)), dma((n - 1,)),
             dma((groups,)), dma((groups,)),
-            dma((2, n - 1)), dma((2, n - 1)), dma,
+            dma((2, n - 1)), dma((2, n - 1)),
         ],
         compiler_params=pltpu.CompilerParams(
             collective_id=0, has_side_effects=True, vmem_limit_bytes=38 * 2**20

time: 511 us -> 511 us (level)
  no operation moved by 1% of the time
where the time goes in v4:
time: 511 us
  Pallas kernels  504 us (99%)
    pallas_call x1, Pallas kernels, on_device(): pl.pallas_call(functools.partial(kernel, n, groups, model), out_shape=(*(...  495 us
  transfers between devices with their start and end apart: 1, of which 1 were waited for; matrix products, arithmetic and copies ran while one was open for 0% of the time, Pallas kernels for 2%

profile of v4, /device:TPU:0, one launch (start us, length us, event | category | flops | bytes accessed | tf_op | source)
XLA Modules:
  0.0 511.0 jit_solution(16854583358522396178)
XLA Ops:
  0.6 495.2 %shard_map.83 = (bf16[16,176,2048]{2,1,0:T(8,128)(2,1)S(1)}, bf16[16,176,2048]{2,1,0:T(8,128)(2,1)S(1)}, f32[16,176]{1,0:T(8,128)S(1)}, f32[16,176]{1,0:T(8,128)...) custom-call(f32[16,256]{1,0:T(8,128)} %bitcast.6, f32[1,256]{1,0:T(1,128)} %bitcast.7, ...), custom_call_target="tpu_custom_call" | custom-call | tf_op jit(solution)/shard_map/pallas_call | solution.py:376
  495.9 2.0 collective-permute-start
  497.9 8.1 %shard_map.84 = (bf16[16,176,2048]{2,1,0:T(8,128)(2,1)}, bf16[16,176,2048]{2,1,0:T(8,128)(2,1)}, f32[16,176]{1,0:T(8,128)}, f32[16,176]{1,0:T(8,128)}, bf16[64,2048]{1,0:T(8,128)(2,1)}) custom-call(bf16[16,176,2048]{2,1,0:T(8,128)(2,1)S(1)} %get-tuple-element.16.refs_0_, bf16[16,176,2048]{2,1,0:T(8,128)(2,1)S(1)} %get-tuple-element.17.refs_1_, ...), custom_call_target="tpu_custom_call" | custom-call | flops 400000000 | bytes 46137344 | tf_op jit(solution)/shard_map/pallas_call | solution.py:413
  506.0 4.2 collective-permute-done.got_ref
  510.3 0.7 shard_map.85
Async XLA Ops:
  495.9 14.4 %collective-permute-start = (bf16[3,176,256]{2,1,0:T(8,128)(2,1)S(1)}, bf16[3,176,256]{2,1,0:T(8,128)(2,1)S(1)}, u32[]{:S(2)}, u32[]{:S(2)}) collective-permute-start(bf16[3,176,256]{2,1,0:T(8,128)(2,1)S(1)} %get-tuple-element.23), channel_id=1, source_target_pairs={{0,4},{1,5},{2,6},{3,7},{4,0},{5,1},{6,2},{7,3},{8,12},{9,13},{10,... | collective-permute-start | bytes 811016 | tf_op jit(solution)/shard_map/ppermute | solution.py:410
